TPU v7x, 256 devices: a whole 4x4x8 slice. The times are simulated.
256 devices in a mesh: shard: 64 (over z, x, core), model: 4 (over y).
Axes of the slice: x: 4, y: 4, z: 8, core: 2. Of those that a mesh axis runs over, the one named last changes fastest.
Arguments:
- grad_stack: float32 [512, 128, 2048], P(None, 'shard', 'model'), may hold values from -6 to 6
- moment_stack: float32 [512, 128, 2048], P(None, 'shard', 'model'), may hold values from -6 to 6
- weight_stack: float32 [512, 128, 2048], P(None, 'shard', 'model'), may hold values from -0.1875 to 0.1875
Outputs:
- new_weights: float32 [512, 128, 2048], P(None, 'shard', 'model')
- new_momentum: float32 [512, 128, 2048], P(None, 'shard', 'model')
All inputs are finite; a program needn't handle non-finite values.
Results may differ from a plain program's by a relative error of at most 0.00021.
Values sent between devices are 32-bit elements; how exact they have to be, the bound alone decides.
A program may use at most 64 MiB of HBM per device.

v0:
```python
import jax
import jax.numpy as jnp
from jax import lax
from jax.sharding import PartitionSpec as P

ITERS = 5
hold_rate = 0.95
learn_rate = 1.0
decay_rate = 0.1


def on_device(grad_stack, moment_stack, weight_stack):
    new_momentum = hold_rate * moment_stack + grad_stack
    moved = lax.all_to_all(new_momentum, "shard", split_axis=0, concat_axis=1, tiled=True)
    whole = lax.all_to_all(moved, "model", split_axis=0, concat_axis=2, tiled=True)
    iterate = whole * lax.rsqrt(jnp.sum(whole * whole, axis=(1, 2), keepdims=True) + 1e-06)
    for step in range(ITERS):
        gram = jnp.einsum("mik,mjk->mij", iterate, iterate, precision=lax.Precision.HIGHEST)
        mixed = -4.775 * gram + 2.0315 * jnp.einsum(
            "mij,mjk->mik", gram, gram, precision=lax.Precision.HIGHEST
        )
        iterate = 3.4445 * iterate + jnp.einsum(
            "mij,mjk->mik", mixed, iterate, precision=lax.Precision.HIGHEST
        )
    iterate = lax.all_to_all(iterate, "model", split_axis=2, concat_axis=0, tiled=True)
    back = lax.all_to_all(iterate, "shard", split_axis=1, concat_axis=0, tiled=True)
    new_weights = (1.0 - learn_rate * decay_rate) * weight_stack - learn_rate * back
    return (new_weights, new_momentum)


def solution(mesh):
    in_specs = (P(None, "shard", "model"), P(None, "shard", "model"), P(None, "shard", "model"))
    out_specs = (P(None, "shard", "model"), P(None, "shard", "model"))
    return jax.shard_map(
        on_device, mesh=mesh, in_specs=in_specs, out_specs=out_specs, check_vma=False
    )
```

profile of v0, /device:TPU:2, one launch (start us, length us, event | category | flops | bytes accessed | tf_op | source)
XLA Modules:
  0.0 220.1 jit_solution(1098745697749330971)
XLA Ops:
  0.6 3.7 %multiply_add_fusion = f32[512,2,512]{2,1,0:T(2,128)S(1)} fusion(f32[512,2,512]{2,1,0:T(2,128)} %param.3, f32[512,2,512]{2,1,0:T(2,128)} %param.4), kind=kLoop, calls=%fused_computation.9 | loop fusion | flops 1048576 | bytes 6291456 | tf_op jit(solution)/shard_map/add | solution.py:13
  4.3 0.0 copy-start
  4.3 63.1 %all_to_all.72 = f32[512,2,512]{2,1,0:T(2,128)S(1)} all-to-all(f32[512,2,512]{2,1,0:T(2,128)S(1)} %multiply_add_fusion), channel_id=1, replica_groups=mesh['shard'=64,'model'=4] {'shard'}, dimensions={0} | all-to-all | bytes 4194304 | tf_op jit(solution)/shard_map/all_to_all | solution.py:14
  67.4 0.4 copy.46
  67.8 0.0 copy-done
  67.8 0.2 copy.31
  68.0 1.2 copy.32
  69.2 29.1 %all_to_all.73 = f32[8,128,512]{2,1,0:T(8,128)S(1)} all-to-all(f32[8,128,512]{2,1,0:T(8,128)S(1)} %copy.32), channel_id=1, replica_groups=mesh['shard'=64,'model'=4] {'model'}, dimensions={0} | all-to-all | bytes 4194304 | tf_op jit(solution)/shard_map/all_to_all | solution.py:15
  98.3 0.4 multiply_reduce_fusion
  98.7 0.2 copy.40
  98.9 2.3 %fusion = f32[2,128,128]{2,1,0:T(8,128)S(1)} fusion(f32[2,128,2048]{2,1,0:T(8,128)S(1)} %bitcast.47, f32[2]{0:T(128)S(1)} %add_rsqrt_fusion), kind=kOutput, calls=%fused_computation.10 | convolution fusion | flops 805830656 | bytes 2228232 | tf_op jit(solution)/shard_map/mik,mjk->mij/dot_general | solution.py:18
  101.2 0.3 fusion.7
  101.5 2.1 convolution_add_fusion.4
  103.6 2.0 fusion.10
  105.7 0.3 fusion.6
  105.9 2.1 convolution_add_fusion.3
  108.1 2.0 fusion.11
  110.1 0.3 fusion.5
  110.4 2.3 %convolution_add_fusion.2 = f32[2,128,2048]{2,1,0:T(8,128)S(1)} fusion(f32[2,128,128]{2,1,0:T(8,128)S(1)} %fusion.5, f32[2,128,2048]{2,1,0:T(8,128)S(1)} %convolution_add_fusion.3), kind=kOutput, calls=%fused_computation.2 | convolution fusion | flops 806354944 | bytes 4325376 | tf_op jit(solution)/shard_map/mij,mjk->mik/dot_general | solution.py:22
  112.7 2.0 fusion.12
  114.8 0.3 fusion.4
  115.0 2.1 convolution_add_fusion.1
  117.1 2.0 fusion.13
  119.2 0.3 fusion.3
  119.4 2.1 convolution_add_fusion
  121.5 2.3 %copy.34 = f32[2,128,2048]{1,0,2:T(2,128)} copy(f32[2,128,2048]{2,1,0:T(8,128)S(1)} %convolution_add_fusion) | data formatting | bytes 4194304 | tf_op jit(solution)/shard_map/add | solution.py:22
  123.9 27.5 %all_to_all.74 = f32[2,128,2048]{1,0,2:T(2,128)S(1)} all-to-all(f32[2,128,2048]{1,0,2:T(2,128)} %copy.34), channel_id=1, replica_groups=mesh['shard'=64,'model'=4] {'model'}, dimensions={2} | all-to-all | bytes 4194304 | tf_op jit(solution)/shard_map/all_to_all | solution.py:25
  151.4 0.1 copy.35
  151.5 1.8 copy.36
  153.3 2.8 %copy.37 = f32[8,128,512]{2,0,1:T(8,128)S(1)} copy(f32[8,128,512]{2,1,0:T(8,128)} %bitcast.55) | data formatting | bytes 4194304 | tf_op jit(solution)/shard_map/all_to_all | solution.py:25
  156.1 0.0 copy-start.1
  156.2 60.4 %all_to_all.75 = f32[8,128,512]{2,0,1:T(8,128)S(1)} all-to-all(f32[8,128,512]{2,0,1:T(8,128)S(1)} %copy.37), channel_id=1, replica_groups=mesh['shard'=64,'model'=4] {'shard'}, dimensions={1} | all-to-all | bytes 4194304 | tf_op jit(solution)/shard_map/all_to_all | solution.py:26
  216.6 0.0 copy-done.1
  216.6 0.6 bitcast_subtract_fusion
  217.2 2.9 %copy.39 = f32[512,2,512]{2,1,0:T(2,128)} copy(f32[512,2,512]{2,0,1:T(8,128)S(1)} %bitcast_subtract_fusion) | data formatting | bytes 4194304
  (1 shorter events, 0.0 us)
Async XLA Ops:
  4.3 63.5 %copy-start = (f32[512,2,512]{2,1,0:T(2,128)}, f32[512,2,512]{2,1,0:T(2,128)S(1)}, u32[]{:S(2)}) copy-start(f32[512,2,512]{2,1,0:T(2,128)S(1)} %multiply_add_fusion) | copy-start | bytes 6291460
  156.1 60.5 %copy-start.1 = (f32[512,2,512]{2,1,0:T(2,128)S(1)}, f32[512,2,512]{2,1,0:T(2,128)}, u32[]{:S(2)}) copy-start(f32[512,2,512]{2,1,0:T(2,128)} %param.5) | copy-start | bytes 6291460
where the time goes:
time: 220 us
  blocking collectives  180 us (82%)
  matrix products  22.5 us (10%)
  local copies, waits for them, and re-layouts  12.1 us (6%)
  other arithmetic  4.62 us (2%)
    all_to_all x1, blocking collectives, on_device(): lax.all_to_all(new_momentum, 'shard', split_axis=0, concat_axis=1, tiled=...  63.1 us
    all_to_all x1, blocking collectives, on_device(): lax.all_to_all(iterate, 'shard', split_axis=1, concat_axis=0, tiled=True)  60.4 us
    all_to_all x1, blocking collectives, on_device(): lax.all_to_all(moved, 'model', split_axis=0, concat_axis=2, tiled=True)  29.1 us
    all_to_all x1, blocking collectives, on_device(): lax.all_to_all(iterate, 'model', split_axis=2, concat_axis=0, tiled=True)  27.5 us
    dot_general x5, matrix products, on_device(): jnp.einsum('mij,mjk->mik', mixed, iterate, precision=lax.Precision.HIGHEST)  10.7 us
    dot_general x5, matrix products, on_device(): jnp.einsum('mik,mjk->mij', iterate, iterate, precision=lax.Precision.HIGH...  10.4 us
    all_to_all x3, local copies, waits for them, and re-layouts, on_device(): lax.all_to_all(iterate, 'model', split_axis=2, concat_axis=0, tiled=True)  4.76 us

commit v1 on v0

--- a/solution.py
+++ b/solution.py
@@ -23,7 +23,12 @@
             "mij,mjk->mik", mixed, iterate, precision=lax.Precision.HIGHEST
         )
     iterate = lax.all_to_all(iterate, "model", split_axis=2, concat_axis=0, tiled=True)
-    back = lax.all_to_all(iterate, "shard", split_axis=1, concat_axis=0, tiled=True)
+    back = jnp.concatenate(
+        lax.all_to_all(
+            jnp.stack(jnp.split(iterate, lax.axis_size("shard"), axis=1)), "shard", 0, 0
+        ),
+        axis=0,
+    )
     new_weights = (1.0 - learn_rate * decay_rate) * weight_stack - learn_rate * back
     return (new_weights, new_momentum)
 

time: 220 us -> 249 us (1.13)
  local copies, waits for them, and re-layouts: 12.1 us -> 36.9 us
  other arithmetic: 4.62 us -> 7.29 us
    unnamed x5 -> x69, local copies, waits for them, and re-layouts: 2.95 us -> 30.5 us
    all_to_all x3 -> x2, local copies, waits for them, and re-layouts: 4.76 us -> 1.95 us  [on_device(): lax.all_to_all(iterate, 'model', split_axis=2, concat_axis=0, tiled=True)]
    sub x1, other arithmetic: 0.59 us -> 3.25 us  [on_device(): (1.0 - learn_rate * decay_rate) * weight_stack - learn_rate * back]
where the time goes in v1:
time: 249 us; the launch traced here: 248 us
  blocking collectives  180 us (72%)
  local copies, waits for them, and re-layouts  36.9 us (15%)
  matrix products  22.5 us (9%)
  other arithmetic  7.29 us (3%)
    all_to_all x1, blocking collectives, on_device(): lax.all_to_all(new_momentum, 'shard', split_axis=0, concat_axis=1, tiled=...  63.1 us
    all_to_all x1, blocking collectives, on_device(): lax.all_to_all(jnp.stack(jnp.split(iterate, lax.axis_size('shard'), axis=...  60.4 us
    unnamed x69, local copies, waits for them, and re-layouts  30.5 us
    all_to_all x1, blocking collectives, on_device(): lax.all_to_all(moved, 'model', split_axis=0, concat_axis=2, tiled=True)  29.1 us
    all_to_all x1, blocking collectives, on_device(): lax.all_to_all(iterate, 'model', split_axis=2, concat_axis=0, tiled=True)  27.5 us
    dot_general x5, matrix products, on_device(): jnp.einsum('mij,mjk->mik', mixed, iterate, precision=lax.Precision.HIGHEST)  10.7 us
    dot_general x5, matrix products, on_device(): jnp.einsum('mik,mjk->mij', iterate, iterate, precision=lax.Precision.HIGH...  10.4 us

profile of v1, /device:TPU:2, one launch (start us, length us, event | category | flops | bytes accessed | tf_op | source)
XLA Modules:
  0.0 247.8 jit_solution(17410104126802785605)
XLA Ops:
  0.6 3.7 %multiply_add_fusion = f32[512,2,512]{2,1,0:T(2,128)S(1)} fusion(f32[512,2,512]{2,1,0:T(2,128)} %param.3, f32[512,2,512]{2,1,0:T(2,128)} %param.4), kind=kLoop, calls=%fused_computation.8 | loop fusion | flops 1048576 | bytes 6291456 | tf_op jit(solution)/shard_map/add | solution.py:13
  4.3 0.0 copy-start
  4.3 63.1 %all_to_all.59 = f32[512,2,512]{2,1,0:T(2,128)S(1)} all-to-all(f32[512,2,512]{2,1,0:T(2,128)S(1)} %multiply_add_fusion), channel_id=1, replica_groups=mesh['shard'=64,'model'=4] {'shard'}, dimensions={0} | all-to-all | bytes 4194304 | tf_op jit(solution)/shard_map/all_to_all | solution.py:14
  67.4 0.4 copy.29
  67.8 0.2 copy.21
  68.0 1.2 copy.22
  69.2 29.1 %all_to_all.60 = f32[8,128,512]{2,1,0:T(8,128)S(1)} all-to-all(f32[8,128,512]{2,1,0:T(8,128)S(1)} %copy.22), channel_id=1, replica_groups=mesh['shard'=64,'model'=4] {'model'}, dimensions={0} | all-to-all | bytes 4194304 | tf_op jit(solution)/shard_map/all_to_all | solution.py:15
  98.3 0.4 multiply_reduce_fusion
  98.7 0.2 copy.27
  98.9 2.3 fusion
  101.2 0.3 fusion.7
  101.5 2.1 convolution_add_fusion.4
  103.6 2.0 fusion.10
  105.7 0.3 fusion.6
  105.9 2.1 convolution_add_fusion.3
  108.1 2.0 fusion.11
  110.1 0.3 fusion.5
  110.4 2.3 convolution_add_fusion.2
  112.7 2.0 fusion.12
  114.8 0.3 fusion.4
  115.0 2.1 convolution_add_fusion.1
  117.1 2.0 fusion.13
  119.2 0.3 fusion.3
  119.4 2.1 convolution_add_fusion
  121.5 2.3 copy.24
  123.9 27.5 %all_to_all.61 = f32[2,128,2048]{1,0,2:T(2,128)S(1)} all-to-all(f32[2,128,2048]{1,0,2:T(2,128)} %copy.24), channel_id=1, replica_groups=mesh['shard'=64,'model'=4] {'model'}, dimensions={2} | all-to-all | bytes 4194304 | tf_op jit(solution)/shard_map/all_to_all | solution.py:25
  151.4 0.1 copy.25
  151.5 1.8 copy.26
  153.3 1.1 constant_dynamic-update-slice_fusion.63
  154.4 0.9 constant_dynamic-update-slice_fusion.62
  155.3 0.9 constant_dynamic-update-slice_fusion.61
  156.3 0.9 constant_dynamic-update-slice_fusion.60
  157.2 0.9 constant_dynamic-update-slice_fusion.59
  158.1 0.9 constant_dynamic-update-slice_fusion.58
  159.0 0.9 constant_dynamic-update-slice_fusion.57
  160.0 0.9 constant_dynamic-update-slice_fusion.56
  160.9 0.9 constant_dynamic-update-slice_fusion.55
  161.8 0.9 constant_dynamic-update-slice_fusion.54
  162.8 0.9 constant_dynamic-update-slice_fusion.53
  163.7 0.9 constant_dynamic-update-slice_fusion.52
  164.6 0.9 constant_dynamic-update-slice_fusion.51
  165.5 0.9 constant_dynamic-update-slice_fusion.50
  166.5 0.9 constant_dynamic-update-slice_fusion.49
  167.4 0.9 constant_dynamic-update-slice_fusion.48
  168.3 0.9 constant_dynamic-update-slice_fusion.47
  169.3 0.9 constant_dynamic-update-slice_fusion.46
  170.2 0.9 constant_dynamic-update-slice_fusion.45
  171.1 0.9 constant_dynamic-update-slice_fusion.44
  172.0 0.9 constant_dynamic-update-slice_fusion.43
  173.0 0.9 constant_dynamic-update-slice_fusion.42
  173.9 0.9 constant_dynamic-update-slice_fusion.41
  174.8 0.9 constant_dynamic-update-slice_fusion.40
  175.8 0.9 constant_dynamic-update-slice_fusion.39
  176.7 0.9 constant_dynamic-update-slice_fusion.38
  177.6 0.9 constant_dynamic-update-slice_fusion.37
  178.5 0.9 constant_dynamic-update-slice_fusion.36
  179.5 0.9 constant_dynamic-update-slice_fusion.35
  180.4 0.9 constant_dynamic-update-slice_fusion.34
  181.3 0.9 constant_dynamic-update-slice_fusion.33
  182.3 0.9 constant_dynamic-update-slice_fusion.32
  184.1 0.0 copy-start.2
  184.1 60.4 %all_to_all.62 = f32[64,8,2,512]{3,2,1,0:T(2,128)S(1)} all-to-all(f32[64,8,2,512]{3,2,1,0:T(2,128)S(1)} %constant_dynamic-update-slice_fusion), channel_id=1, replica_groups=mesh['shard'=64,'model'=4] {'shard'}, dimensions={0} | all-to-all | bytes 4194304 | tf_op jit(solution)/shard_map/all_to_all | solution.py:27
  244.5 0.0 copy-done.2
  244.5 3.3 %bitcast_subtract_fusion = f32[512,2,512]{2,1,0:T(2,128)} fusion(f32[64,8,2,512]{3,2,1,0:T(2,128)S(1)} %all_to_all.62, f32[512,2,512]{2,1,0:T(2,128)S(1)} %copy-done.2), kind=kLoop, calls=%fused_computation.5 | loop fusion | flops 1048576 | bytes 6291456 | tf_op jit(solution)/shard_map/sub | solution.py:32
  (36 shorter events, 0.7 us)
Async XLA Ops:
  4.3 63.5 %copy-start = (f32[512,2,512]{2,1,0:T(2,128)}, f32[512,2,512]{2,1,0:T(2,128)S(1)}, u32[]{:S(2)}) copy-start(f32[512,2,512]{2,1,0:T(2,128)S(1)} %multiply_add_fusion) | copy-start | bytes 6291460
  153.3 29.9 %copy-start.1 = (f32[4,2,128,512]{3,2,1,0:T(8,128)S(1)}, f32[4,2,128,512]{3,2,1,0:T(8,128)}, u32[]{:S(2)}) copy-start(f32[4,2,128,512]{3,2,1,0:T(8,128)} %copy.26) | copy-start | bytes 6291460
  184.1 60.5 %copy-start.2 = (f32[512,2,512]{2,1,0:T(2,128)S(1)}, f32[512,2,512]{2,1,0:T(2,128)}, u32[]{:S(2)}) copy-start(f32[512,2,512]{2,1,0:T(2,128)} %param.5) | copy-start | bytes 6291460
